TPU v7x, 32 devices: a whole 2x2x4 slice. The times are simulated.
32 devices in a mesh: ctx: 16 (over z, y, core), head: 2 (over x).
Axes of the slice: x: 2, y: 2, z: 4, core: 2. Of those that a mesh axis runs over, the one named last changes fastest.
Arguments:
- queries: bfloat16 [1792, 16384], P('ctx', 'head'), may hold values from -120 to 120
- keys: bfloat16 [1792, 1024], P('ctx', 'head'), may hold values from -4.5 to 4.5
- values: bfloat16 [1792, 1024], P('ctx', 'head'), may hold values from -6 to 6
- span_pos: int32 [32], replicated, may hold values from 0 to 31, as said below
Outputs:
- attended: bfloat16 [1792, 16384], P(('ctx', 'head'))
Inputs may be any that keep to these rules, and one draw needn't show every extreme that they name: `span_pos`: a permutation of 0 to 31; entries 2b and 2b + 1 sum to 31.
All inputs are finite; a program needn't handle non-finite values.
Results may differ from a plain program's by a relative error of at most 0.0049.
Values may be sent and summed in bfloat16 or wider, within the bound.
A program may use at most 64 MiB of HBM per device.

v0:
```python
import jax
import jax.numpy as jnp
from jax import lax
from jax.sharding import PartitionSpec as P

HEAD_DIM = 128


NEG_FLOOR = -1e30


def passed_along(value, axis, steps):
    count = lax.axis_size(axis)
    pairs = [(source, (source + steps) % count) for source in range(count)]
    return lax.ppermute(value, axis, pairs)


def block_partial(query_block, query_pos, key_block, value_block, key_pos):
    scale = query_block.shape[-1] ** (-0.5)
    scores = (
        jnp.einsum("qgjd,kgd->gjqk", query_block, key_block, preferred_element_type=jnp.float32)
        * scale
    )
    visible = key_pos[None, :] <= query_pos[:, None]
    row_max = jnp.max(jnp.where(visible, scores, NEG_FLOOR), axis=-1)
    weights = jnp.where(visible, jnp.exp(scores - row_max[..., None]), 0.0)
    totals = jnp.sum(weights, axis=-1)
    product = jnp.einsum(
        "gjqk,kgd->qgjd",
        weights.astype(jnp.bfloat16),
        value_block,
        preferred_element_type=jnp.float32,
    )
    totals_rows = jnp.transpose(totals, (2, 0, 1))
    max_rows = jnp.transpose(row_max, (2, 0, 1))
    seen = totals_rows > 0.0
    safe_totals = jnp.where(seen, totals_rows, 1.0)
    partial_value = jnp.where(seen[..., None], product / safe_totals[..., None], 0.0).astype(
        jnp.bfloat16
    )
    log_total = jnp.where(seen, max_rows + jnp.log(safe_totals), NEG_FLOOR)
    return (partial_value, log_total)


def merge_parts(parts, log_totals):
    top = jnp.max(log_totals, axis=0)
    factors = jnp.exp(log_totals - top[None])
    denom = jnp.sum(factors, axis=0)
    numer = jnp.sum(factors[..., None] * parts.astype(jnp.float32), axis=0)
    return (numer / denom[..., None]).astype(jnp.bfloat16)


def per_device(queries, keys, values, span_pos):
    row_count = queries.shape[0]
    span_len = row_count // 2
    kv_local = keys.shape[1] // HEAD_DIM
    group = queries.shape[1] // HEAD_DIM // kv_local
    cycle_size = lax.axis_size("ctx")
    my_index = lax.axis_index("ctx")
    offsets = jnp.arange(span_len, dtype=jnp.int32)
    positions = (span_pos[:, None] * span_len + offsets[None, :]).reshape(-1)

    def block_positions(source):
        slot = (source + cycle_size) % cycle_size
        return lax.dynamic_slice_in_dim(positions, slot * row_count, row_count)

    my_pos = block_positions(my_index)
    own_queries = queries.reshape(row_count, kv_local, group, HEAD_DIM)
    own_keys = keys.reshape(row_count, kv_local, HEAD_DIM)
    own_values = values.reshape(row_count, kv_local, HEAD_DIM)
    empty_parts = jnp.zeros((cycle_size, row_count, kv_local, group, HEAD_DIM), jnp.bfloat16)
    empty_logs = jnp.full((cycle_size, row_count, kv_local, group), NEG_FLOOR, jnp.float32)

    def record(buffers, source, partial_value, log_total):
        slot = (source + cycle_size) % cycle_size
        return (
            lax.dynamic_update_slice_in_dim(buffers[0], partial_value[None], slot, 0),
            lax.dynamic_update_slice_in_dim(buffers[1], log_total[None], slot, 0),
        )

    def visit_keys(buffers, visiting, source):
        partial_value, log_total = block_partial(
            own_queries, my_pos, visiting[0], visiting[1], block_positions(source)
        )
        return record(buffers, source, partial_value, log_total)

    stacked = jnp.stack([own_keys, own_values])

    def key_turn(turn, carry):
        visiting, buffers = carry
        for half in range(2):
            buffers = visit_keys(buffers, visiting, my_index - 2 * turn - half)
            visiting = passed_along(visiting, "ctx", 1)
        return (visiting, buffers)

    visiting, buffers = lax.fori_loop(
        0, cycle_size // 2, key_turn, (stacked, (empty_parts, empty_logs))
    )
    parts, log_totals = buffers
    merged = merge_parts(parts, log_totals).reshape(row_count, kv_local * group * HEAD_DIM)
    return lax.all_to_all(merged, "head", split_axis=0, concat_axis=1, tiled=True)


def solution(mesh):
    in_specs = (P("ctx", "head"), P("ctx", "head"), P("ctx", "head"), P())
    out_specs = P(("ctx", "head"), None)
    return jax.shard_map(
        per_device, mesh=mesh, in_specs=in_specs, out_specs=out_specs, check_vma=False
    )
```

profile of v0, /device:TPU:0, one launch (start us, length us, event | category | flops | bytes accessed | tf_op | source)
XLA Modules:
  0.0 260.7 jit_solution(14185285849912553800)
XLA Ops:
  4.5 10.2 %broadcast_in_dim.234 = bf16[16,112,4,16,128]{4,1,3,2,0:T(8,128)(2,1)} broadcast(bf16[]{:T(256)} %constant.191.clone.1), dimensions={} | broadcast | bytes 29360130 | tf_op jit(solution)/shard_map/broadcast_in_dim | solution.py:71
  14.7 201.4 %while.21 = (s32[]{:T(128)}, bf16[2,112,4,128]{3,1,2,0:T(8,128)(2,1)S(1)}, bf16[16,112,4,16,128]{4,1,3,2,0:T(8,128)(2,1)}, f32[16,112,4,16]{1,3,2,0:T(8,128)S(1)...) while((s32[]{:T(128)}, ...), condition=%wide.region_5.6_spmd, body=%wide.region_0.5_spmd.sunk | while | flops 845318656 | bytes 30591708 | solution.py:96
  16.8 7.1 %collective-permute-done = bf16[2,112,4,128]{3,1,2,0:T(8,128)(2,1)S(1)} collective-permute-done((bf16[2,112,4,128]{3,1,2,0:T(8,128)(2,1)S(1)}, bf16[2,112,4,128]{3,1,2,0:T(8,128)(2,1)S(1)}, u32[]{:S(2)}, u32[]{:S(2)}) %collective-permute-start) | collective-permute-done | bytes 229408 | tf_op jit(solution)/shard_map/while/body/eval_jaxpr/ppermute | solution.py:15
  27.8 4.9 %bitcast_dynamic-update-slice_fusion.9 = bf16[16,112,4,16,128]{4,1,3,2,0:T(8,128)(2,1)} fusion(bf16[16,112,4,16,128]{4,1,3,2,0:T(8,128)(2,1)} %get-tuple-element.417, s32[]{:T(128)S(6)} %select_n.314, f32[112,4,16]{0,2,1:T(8,128)S(1)} %bitcast_select_fusion.6, f32[4,112,112,16]{2,1,3,0:T(8,128)S(1)} %get-tuple-element.390, ...), kind=kOutput, calls=%fused_computation.21.clone.1 | convolution fusion | flops 211484672 | bytes 5707780 | tf_op jit(solution)/shard_map/while/body/eval_jaxpr/gjqk,kgd->qgjd/dot_general | solution.py:28
  32.7 4.9 %bitcast_dynamic-update-slice_fusion.11 = bf16[16,112,4,16,128]{4,1,3,2,0:T(8,128)(2,1)} fusion(bf16[16,112,4,16,128]{4,1,3,2,0:T(8,128)(2,1)} %bitcast_dynamic-update-slice_fusion.9, s32[]{:T(128)S(6)} %select_n.318, f32[112,4,16]{0,2,1:T(8,128)S(1)} %bitcast_select_fusion.7, f32[4,112,112,16]{2,1,3,0:T(8,128)S(1)} %get-tuple-element.393, ...), kind=kOutput, calls=%fused_computation.20.clone.1 | convolution fusion | flops 211484672 | bytes 5707780 | tf_op jit(solution)/shard_map/while/body/eval_jaxpr/gjqk,kgd->qgjd/dot_general | solution.py:28
  42.4 6.5 %collective-permute-done = bf16[2,112,4,128]{3,1,2,0:T(8,128)(2,1)S(1)} collective-permute-done((bf16[2,112,4,128]{3,1,2,0:T(8,128)(2,1)S(1)}, bf16[2,112,4,128]{3,1,2,0:T(8,128)(2,1)S(1)}, u32[]{:S(2)}, u32[]{:S(2)}) %collective-permute-start) | collective-permute-done | bytes 229408 | tf_op jit(solution)/shard_map/while/body/eval_jaxpr/ppermute | solution.py:15
  52.8 4.9 %bitcast_dynamic-update-slice_fusion.9 = bf16[16,112,4,16,128]{4,1,3,2,0:T(8,128)(2,1)} fusion(bf16[16,112,4,16,128]{4,1,3,2,0:T(8,128)(2,1)} %get-tuple-element.417, s32[]{:T(128)S(6)} %select_n.314, f32[112,4,16]{0,2,1:T(8,128)S(1)} %bitcast_select_fusion.6, f32[4,112,112,16]{2,1,3,0:T(8,128)S(1)} %get-tuple-element.390, ...), kind=kOutput, calls=%fused_computation.21.clone.1 | convolution fusion | flops 211484672 | bytes 5707780 | tf_op jit(solution)/shard_map/while/body/eval_jaxpr/gjqk,kgd->qgjd/dot_general | solution.py:28
  57.7 4.9 %bitcast_dynamic-update-slice_fusion.11 = bf16[16,112,4,16,128]{4,1,3,2,0:T(8,128)(2,1)} fusion(bf16[16,112,4,16,128]{4,1,3,2,0:T(8,128)(2,1)} %bitcast_dynamic-update-slice_fusion.9, s32[]{:T(128)S(6)} %select_n.318, f32[112,4,16]{0,2,1:T(8,128)S(1)} %bitcast_select_fusion.7, f32[4,112,112,16]{2,1,3,0:T(8,128)S(1)} %get-tuple-element.393, ...), kind=kOutput, calls=%fused_computation.20.clone.1 | convolution fusion | flops 211484672 | bytes 5707780 | tf_op jit(solution)/shard_map/while/body/eval_jaxpr/gjqk,kgd->qgjd/dot_general | solution.py:28
  67.5 6.5 %collective-permute-done = bf16[2,112,4,128]{3,1,2,0:T(8,128)(2,1)S(1)} collective-permute-done((bf16[2,112,4,128]{3,1,2,0:T(8,128)(2,1)S(1)}, bf16[2,112,4,128]{3,1,2,0:T(8,128)(2,1)S(1)}, u32[]{:S(2)}, u32[]{:S(2)}) %collective-permute-start) | collective-permute-done | bytes 229408 | tf_op jit(solution)/shard_map/while/body/eval_jaxpr/ppermute | solution.py:15
  77.9 4.9 %bitcast_dynamic-update-slice_fusion.9 = bf16[16,112,4,16,128]{4,1,3,2,0:T(8,128)(2,1)} fusion(bf16[16,112,4,16,128]{4,1,3,2,0:T(8,128)(2,1)} %get-tuple-element.417, s32[]{:T(128)S(6)} %select_n.314, f32[112,4,16]{0,2,1:T(8,128)S(1)} %bitcast_select_fusion.6, f32[4,112,112,16]{2,1,3,0:T(8,128)S(1)} %get-tuple-element.390, ...), kind=kOutput, calls=%fused_computation.21.clone.1 | convolution fusion | flops 211484672 | bytes 5707780 | tf_op jit(solution)/shard_map/while/body/eval_jaxpr/gjqk,kgd->qgjd/dot_general | solution.py:28
  82.8 4.9 %bitcast_dynamic-update-slice_fusion.11 = bf16[16,112,4,16,128]{4,1,3,2,0:T(8,128)(2,1)} fusion(bf16[16,112,4,16,128]{4,1,3,2,0:T(8,128)(2,1)} %bitcast_dynamic-update-slice_fusion.9, s32[]{:T(128)S(6)} %select_n.318, f32[112,4,16]{0,2,1:T(8,128)S(1)} %bitcast_select_fusion.7, f32[4,112,112,16]{2,1,3,0:T(8,128)S(1)} %get-tuple-element.393, ...), kind=kOutput, calls=%fused_computation.20.clone.1 | convolution fusion | flops 211484672 | bytes 5707780 | tf_op jit(solution)/shard_map/while/body/eval_jaxpr/gjqk,kgd->qgjd/dot_general | solution.py:28
  87.7 3.2 %collective-permute-done.1 = bf16[2,112,4,128]{3,1,2,0:T(8,128)(2,1)S(1)} collective-permute-done((bf16[2,112,4,128]{3,1,2,0:T(8,128)(2,1)S(1)}, bf16[2,112,4,128]{3,1,2,0:T(8,128)(2,1)S(1)}, u32[]{:S(2)}, u32[]{:S(2)}) %collective-permute-start.1) | collective-permute-done | bytes 229408 | tf_op jit(solution)/shard_map/while/body/eval_jaxpr/ppermute | solution.py:15
  92.5 6.5 %collective-permute-done = bf16[2,112,4,128]{3,1,2,0:T(8,128)(2,1)S(1)} collective-permute-done((bf16[2,112,4,128]{3,1,2,0:T(8,128)(2,1)S(1)}, bf16[2,112,4,128]{3,1,2,0:T(8,128)(2,1)S(1)}, u32[]{:S(2)}, u32[]{:S(2)}) %collective-permute-start) | collective-permute-done | bytes 229408 | tf_op jit(solution)/shard_map/while/body/eval_jaxpr/ppermute | solution.py:15
  102.9 4.9 %bitcast_dynamic-update-slice_fusion.9 = bf16[16,112,4,16,128]{4,1,3,2,0:T(8,128)(2,1)} fusion(bf16[16,112,4,16,128]{4,1,3,2,0:T(8,128)(2,1)} %get-tuple-element.417, s32[]{:T(128)S(6)} %select_n.314, f32[112,4,16]{0,2,1:T(8,128)S(1)} %bitcast_select_fusion.6, f32[4,112,112,16]{2,1,3,0:T(8,128)S(1)} %get-tuple-element.390, ...), kind=kOutput, calls=%fused_computation.21.clone.1 | convolution fusion | flops 211484672 | bytes 5707780 | tf_op jit(solution)/shard_map/while/body/eval_jaxpr/gjqk,kgd->qgjd/dot_general | solution.py:28
  107.8 4.9 %bitcast_dynamic-update-slice_fusion.11 = bf16[16,112,4,16,128]{4,1,3,2,0:T(8,128)(2,1)} fusion(bf16[16,112,4,16,128]{4,1,3,2,0:T(8,128)(2,1)} %bitcast_dynamic-update-slice_fusion.9, s32[]{:T(128)S(6)} %select_n.318, f32[112,4,16]{0,2,1:T(8,128)S(1)} %bitcast_select_fusion.7, f32[4,112,112,16]{2,1,3,0:T(8,128)S(1)} %get-tuple-element.393, ...), kind=kOutput, calls=%fused_computation.20.clone.1 | convolution fusion | flops 211484672 | bytes 5707780 | tf_op jit(solution)/shard_map/while/body/eval_jaxpr/gjqk,kgd->qgjd/dot_general | solution.py:28
  112.7 3.3 %collective-permute-done.1 = bf16[2,112,4,128]{3,1,2,0:T(8,128)(2,1)S(1)} collective-permute-done((bf16[2,112,4,128]{3,1,2,0:T(8,128)(2,1)S(1)}, bf16[2,112,4,128]{3,1,2,0:T(8,128)(2,1)S(1)}, u32[]{:S(2)}, u32[]{:S(2)}) %collective-permute-start.1) | collective-permute-done | bytes 229408 | tf_op jit(solution)/shard_map/while/body/eval_jaxpr/ppermute | solution.py:15
  117.6 6.5 %collective-permute-done = bf16[2,112,4,128]{3,1,2,0:T(8,128)(2,1)S(1)} collective-permute-done((bf16[2,112,4,128]{3,1,2,0:T(8,128)(2,1)S(1)}, bf16[2,112,4,128]{3,1,2,0:T(8,128)(2,1)S(1)}, u32[]{:S(2)}, u32[]{:S(2)}) %collective-permute-start) | collective-permute-done | bytes 229408 | tf_op jit(solution)/shard_map/while/body/eval_jaxpr/ppermute | solution.py:15
  127.9 4.9 %bitcast_dynamic-update-slice_fusion.9 = bf16[16,112,4,16,128]{4,1,3,2,0:T(8,128)(2,1)} fusion(bf16[16,112,4,16,128]{4,1,3,2,0:T(8,128)(2,1)} %get-tuple-element.417, s32[]{:T(128)S(6)} %select_n.314, f32[112,4,16]{0,2,1:T(8,128)S(1)} %bitcast_select_fusion.6, f32[4,112,112,16]{2,1,3,0:T(8,128)S(1)} %get-tuple-element.390, ...), kind=kOutput, calls=%fused_computation.21.clone.1 | convolution fusion | flops 211484672 | bytes 5707780 | tf_op jit(solution)/shard_map/while/body/eval_jaxpr/gjqk,kgd->qgjd/dot_general | solution.py:28
  132.8 4.9 %bitcast_dynamic-update-slice_fusion.11 = bf16[16,112,4,16,128]{4,1,3,2,0:T(8,128)(2,1)} fusion(bf16[16,112,4,16,128]{4,1,3,2,0:T(8,128)(2,1)} %bitcast_dynamic-update-slice_fusion.9, s32[]{:T(128)S(6)} %select_n.318, f32[112,4,16]{0,2,1:T(8,128)S(1)} %bitcast_select_fusion.7, f32[4,112,112,16]{2,1,3,0:T(8,128)S(1)} %get-tuple-element.393, ...), kind=kOutput, calls=%fused_computation.20.clone.1 | convolution fusion | flops 211484672 | bytes 5707780 | tf_op jit(solution)/shard_map/while/body/eval_jaxpr/gjqk,kgd->qgjd/dot_general | solution.py:28
  137.7 3.3 %collective-permute-done.1 = bf16[2,112,4,128]{3,1,2,0:T(8,128)(2,1)S(1)} collective-permute-done((bf16[2,112,4,128]{3,1,2,0:T(8,128)(2,1)S(1)}, bf16[2,112,4,128]{3,1,2,0:T(8,128)(2,1)S(1)}, u32[]{:S(2)}, u32[]{:S(2)}) %collective-permute-start.1) | collective-permute-done | bytes 229408 | tf_op jit(solution)/shard_map/while/body/eval_jaxpr/ppermute | solution.py:15
  142.6 6.5 %collective-permute-done = bf16[2,112,4,128]{3,1,2,0:T(8,128)(2,1)S(1)} collective-permute-done((bf16[2,112,4,128]{3,1,2,0:T(8,128)(2,1)S(1)}, bf16[2,112,4,128]{3,1,2,0:T(8,128)(2,1)S(1)}, u32[]{:S(2)}, u32[]{:S(2)}) %collective-permute-start) | collective-permute-done | bytes 229408 | tf_op jit(solution)/shard_map/while/body/eval_jaxpr/ppermute | solution.py:15
  153.0 4.9 %bitcast_dynamic-update-slice_fusion.9 = bf16[16,112,4,16,128]{4,1,3,2,0:T(8,128)(2,1)} fusion(bf16[16,112,4,16,128]{4,1,3,2,0:T(8,128)(2,1)} %get-tuple-element.417, s32[]{:T(128)S(6)} %select_n.314, f32[112,4,16]{0,2,1:T(8,128)S(1)} %bitcast_select_fusion.6, f32[4,112,112,16]{2,1,3,0:T(8,128)S(1)} %get-tuple-element.390, ...), kind=kOutput, calls=%fused_computation.21.clone.1 | convolution fusion | flops 211484672 | bytes 5707780 | tf_op jit(solution)/shard_map/while/body/eval_jaxpr/gjqk,kgd->qgjd/dot_general | solution.py:28
  157.9 4.9 %bitcast_dynamic-update-slice_fusion.11 = bf16[16,112,4,16,128]{4,1,3,2,0:T(8,128)(2,1)} fusion(bf16[16,112,4,16,128]{4,1,3,2,0:T(8,128)(2,1)} %bitcast_dynamic-update-slice_fusion.9, s32[]{:T(128)S(6)} %select_n.318, f32[112,4,16]{0,2,1:T(8,128)S(1)} %bitcast_select_fusion.7, f32[4,112,112,16]{2,1,3,0:T(8,128)S(1)} %get-tuple-element.393, ...), kind=kOutput, calls=%fused_computation.20.clone.1 | convolution fusion | flops 211484672 | bytes 5707780 | tf_op jit(solution)/shard_map/while/body/eval_jaxpr/gjqk,kgd->qgjd/dot_general | solution.py:28
  162.8 3.3 %collective-permute-done.1 = bf16[2,112,4,128]{3,1,2,0:T(8,128)(2,1)S(1)} collective-permute-done((bf16[2,112,4,128]{3,1,2,0:T(8,128)(2,1)S(1)}, bf16[2,112,4,128]{3,1,2,0:T(8,128)(2,1)S(1)}, u32[]{:S(2)}, u32[]{:S(2)}) %collective-permute-start.1) | collective-permute-done | bytes 229408 | tf_op jit(solution)/shard_map/while/body/eval_jaxpr/ppermute | solution.py:15
  167.6 6.5 %collective-permute-done = bf16[2,112,4,128]{3,1,2,0:T(8,128)(2,1)S(1)} collective-permute-done((bf16[2,112,4,128]{3,1,2,0:T(8,128)(2,1)S(1)}, bf16[2,112,4,128]{3,1,2,0:T(8,128)(2,1)S(1)}, u32[]{:S(2)}, u32[]{:S(2)}) %collective-permute-start) | collective-permute-done | bytes 229408 | tf_op jit(solution)/shard_map/while/body/eval_jaxpr/ppermute | solution.py:15
  178.0 4.9 %bitcast_dynamic-update-slice_fusion.9 = bf16[16,112,4,16,128]{4,1,3,2,0:T(8,128)(2,1)} fusion(bf16[16,112,4,16,128]{4,1,3,2,0:T(8,128)(2,1)} %get-tuple-element.417, s32[]{:T(128)S(6)} %select_n.314, f32[112,4,16]{0,2,1:T(8,128)S(1)} %bitcast_select_fusion.6, f32[4,112,112,16]{2,1,3,0:T(8,128)S(1)} %get-tuple-element.390, ...), kind=kOutput, calls=%fused_computation.21.clone.1 | convolution fusion | flops 211484672 | bytes 5707780 | tf_op jit(solution)/shard_map/while/body/eval_jaxpr/gjqk,kgd->qgjd/dot_general | solution.py:28
  183.0 4.9 %bitcast_dynamic-update-slice_fusion.11 = bf16[16,112,4,16,128]{4,1,3,2,0:T(8,128)(2,1)} fusion(bf16[16,112,4,16,128]{4,1,3,2,0:T(8,128)(2,1)} %bitcast_dynamic-update-slice_fusion.9, s32[]{:T(128)S(6)} %select_n.318, f32[112,4,16]{0,2,1:T(8,128)S(1)} %bitcast_select_fusion.7, f32[4,112,112,16]{2,1,3,0:T(8,128)S(1)} %get-tuple-element.393, ...), kind=kOutput, calls=%fused_computation.20.clone.1 | convolution fusion | flops 211484672 | bytes 5707780 | tf_op jit(solution)/shard_map/while/body/eval_jaxpr/gjqk,kgd->qgjd/dot_general | solution.py:28
  192.7 6.5 %collective-permute-done = bf16[2,112,4,128]{3,1,2,0:T(8,128)(2,1)S(1)} collective-permute-done((bf16[2,112,4,128]{3,1,2,0:T(8,128)(2,1)S(1)}, bf16[2,112,4,128]{3,1,2,0:T(8,128)(2,1)S(1)}, u32[]{:S(2)}, u32[]{:S(2)}) %collective-permute-start) | collective-permute-done | bytes 229408 | tf_op jit(solution)/shard_map/while/body/eval_jaxpr/ppermute | solution.py:15
  203.1 4.9 %bitcast_dynamic-update-slice_fusion.9 = bf16[16,112,4,16,128]{4,1,3,2,0:T(8,128)(2,1)} fusion(bf16[16,112,4,16,128]{4,1,3,2,0:T(8,128)(2,1)} %get-tuple-element.417, s32[]{:T(128)S(6)} %select_n.314, f32[112,4,16]{0,2,1:T(8,128)S(1)} %bitcast_select_fusion.6, f32[4,112,112,16]{2,1,3,0:T(8,128)S(1)} %get-tuple-element.390, ...), kind=kOutput, calls=%fused_computation.21.clone.1 | convolution fusion | flops 211484672 | bytes 5707780 | tf_op jit(solution)/shard_map/while/body/eval_jaxpr/gjqk,kgd->qgjd/dot_general | solution.py:28
  208.0 4.9 %bitcast_dynamic-update-slice_fusion.11 = bf16[16,112,4,16,128]{4,1,3,2,0:T(8,128)(2,1)} fusion(bf16[16,112,4,16,128]{4,1,3,2,0:T(8,128)(2,1)} %bitcast_dynamic-update-slice_fusion.9, s32[]{:T(128)S(6)} %select_n.318, f32[112,4,16]{0,2,1:T(8,128)S(1)} %bitcast_select_fusion.7, f32[4,112,112,16]{2,1,3,0:T(8,128)S(1)} %get-tuple-element.393, ...), kind=kOutput, calls=%fused_computation.20.clone.1 | convolution fusion | flops 211484672 | bytes 5707780 | tf_op jit(solution)/shard_map/while/body/eval_jaxpr/gjqk,kgd->qgjd/dot_general | solution.py:28
  216.3 20.0 %multiply_reduce_fusion = f32[112,4,16,128]{3,0,2,1:T(8,128)S(1)} fusion(bf16[16,112,4,16,128]{4,1,3,2,0:T(8,128)(2,1)} %get-tuple-element.266, f32[16,112,4,16]{1,3,2,0:T(8,128)S(1)} %get-tuple-element.312), kind=kLoop, calls=%fused_computation.54 | loop fusion | flops 43122688 | bytes 33488896 | tf_op jit(solution)/shard_map/reduce_sum | solution.py:49
  239.7 19.7 %all_to_all.16 = bf16[2,56,8192]{2,1,0:T(8,128)(2,1)S(1)} all-to-all(bf16[2,56,8192]{2,1,0:T(8,128)(2,1)} %convert_element_type.65), channel_id=1, replica_groups=mesh['ctx'=16,'head'=2] {'head'}, dimensions={0} | all-to-all | bytes 3670016 | tf_op jit(solution)/shard_map/all_to_all | solution.py:101
  (113 shorter events, 65.9 us)
Async XLA Ops:
  0.8 3.3 %copy-start = (bf16[112,512]{1,0:T(8,128)(2,1)S(1)}, bf16[112,512]{1,0:T(8,128)(2,1)}, u32[]{:S(2)}) copy-start(bf16[112,512]{1,0:T(8,128)(2,1)} %param.7) | copy-start | bytes 344068
  0.8 3.3 %copy-start.1 = (bf16[112,512]{1,0:T(8,128)(2,1)S(1)}, bf16[112,512]{1,0:T(8,128)(2,1)}, u32[]{:S(2)}) copy-start(bf16[112,512]{1,0:T(8,128)(2,1)} %param.8) | copy-start | bytes 344068
  14.7 9.2 %collective-permute-start = (bf16[2,112,4,128]{3,1,2,0:T(8,128)(2,1)S(1)}, bf16[2,112,4,128]{3,1,2,0:T(8,128)(2,1)S(1)}, u32[]{:S(2)}, u32[]{:S(2)}) collective-permute-start(bf16[2,112,4,128]{3,1,2,0:T(8,128)(2,1)S(1)} %get-tuple-element.416), channel_id=1, source_target_pairs={{0,2},{2,4},{4,6},{6,8},{8,10},{10,12},{12,14},{14,16},{16,18},{18... | collective-permute-start | bytes 688136 | tf_op jit(solution)/shard_map/while/body/eval_jaxpr/ppermute | solution.py:15
  32.7 8.1 %collective-permute-start.1 = (bf16[2,112,4,128]{3,1,2,0:T(8,128)(2,1)S(1)}, bf16[2,112,4,128]{3,1,2,0:T(8,128)(2,1)S(1)}, u32[]{:S(2)}, u32[]{:S(2)}) collective-permute-start(bf16[2,112,4,128]{3,1,2,0:T(8,128)(2,1)S(1)} %collective-permute-done), channel_id=1, source_target_pairs={{0,2},{2,4},{4,6},{6,8},{8,10},{10,12},{12,14},{14,16},{16,18},{18... | collective-permute-start | bytes 688136 | tf_op jit(solution)/shard_map/while/body/eval_jaxpr/ppermute | solution.py:15
  40.8 8.1 %collective-permute-start = (bf16[2,112,4,128]{3,1,2,0:T(8,128)(2,1)S(1)}, bf16[2,112,4,128]{3,1,2,0:T(8,128)(2,1)S(1)}, u32[]{:S(2)}, u32[]{:S(2)}) collective-permute-start(bf16[2,112,4,128]{3,1,2,0:T(8,128)(2,1)S(1)} %get-tuple-element.416), channel_id=1, source_target_pairs={{0,2},{2,4},{4,6},{6,8},{8,10},{10,12},{12,14},{14,16},{16,18},{18... | collective-permute-start | bytes 688136 | tf_op jit(solution)/shard_map/while/body/eval_jaxpr/ppermute | solution.py:15
  57.7 8.1 %collective-permute-start.1 = (bf16[2,112,4,128]{3,1,2,0:T(8,128)(2,1)S(1)}, bf16[2,112,4,128]{3,1,2,0:T(8,128)(2,1)S(1)}, u32[]{:S(2)}, u32[]{:S(2)}) collective-permute-start(bf16[2,112,4,128]{3,1,2,0:T(8,128)(2,1)S(1)} %collective-permute-done), channel_id=1, source_target_pairs={{0,2},{2,4},{4,6},{6,8},{8,10},{10,12},{12,14},{14,16},{16,18},{18... | collective-permute-start | bytes 688136 | tf_op jit(solution)/shard_map/while/body/eval_jaxpr/ppermute | solution.py:15
  65.9 8.1 %collective-permute-start = (bf16[2,112,4,128]{3,1,2,0:T(8,128)(2,1)S(1)}, bf16[2,112,4,128]{3,1,2,0:T(8,128)(2,1)S(1)}, u32[]{:S(2)}, u32[]{:S(2)}) collective-permute-start(bf16[2,112,4,128]{3,1,2,0:T(8,128)(2,1)S(1)} %get-tuple-element.416), channel_id=1, source_target_pairs={{0,2},{2,4},{4,6},{6,8},{8,10},{10,12},{12,14},{14,16},{16,18},{18... | collective-permute-start | bytes 688136 | tf_op jit(solution)/shard_map/while/body/eval_jaxpr/ppermute | solution.py:15
  82.8 8.1 %collective-permute-start.1 = (bf16[2,112,4,128]{3,1,2,0:T(8,128)(2,1)S(1)}, bf16[2,112,4,128]{3,1,2,0:T(8,128)(2,1)S(1)}, u32[]{:S(2)}, u32[]{:S(2)}) collective-permute-start(bf16[2,112,4,128]{3,1,2,0:T(8,128)(2,1)S(1)} %collective-permute-done), channel_id=1, source_target_pairs={{0,2},{2,4},{4,6},{6,8},{8,10},{10,12},{12,14},{14,16},{16,18},{18... | collective-permute-start | bytes 688136 | tf_op jit(solution)/shard_map/while/body/eval_jaxpr/ppermute | solution.py:15
  90.9 8.1 %collective-permute-start = (bf16[2,112,4,128]{3,1,2,0:T(8,128)(2,1)S(1)}, bf16[2,112,4,128]{3,1,2,0:T(8,128)(2,1)S(1)}, u32[]{:S(2)}, u32[]{:S(2)}) collective-permute-start(bf16[2,112,4,128]{3,1,2,0:T(8,128)(2,1)S(1)} %get-tuple-element.416), channel_id=1, source_target_pairs={{0,2},{2,4},{4,6},{6,8},{8,10},{10,12},{12,14},{14,16},{16,18},{18... | collective-permute-start | bytes 688136 | tf_op jit(solution)/shard_map/while/body/eval_jaxpr/ppermute | solution.py:15
  107.8 8.1 %collective-permute-start.1 = (bf16[2,112,4,128]{3,1,2,0:T(8,128)(2,1)S(1)}, bf16[2,112,4,128]{3,1,2,0:T(8,128)(2,1)S(1)}, u32[]{:S(2)}, u32[]{:S(2)}) collective-permute-start(bf16[2,112,4,128]{3,1,2,0:T(8,128)(2,1)S(1)} %collective-permute-done), channel_id=1, source_target_pairs={{0,2},{2,4},{4,6},{6,8},{8,10},{10,12},{12,14},{14,16},{16,18},{18... | collective-permute-start | bytes 688136 | tf_op jit(solution)/shard_map/while/body/eval_jaxpr/ppermute | solution.py:15
  116.0 8.1 %collective-permute-start = (bf16[2,112,4,128]{3,1,2,0:T(8,128)(2,1)S(1)}, bf16[2,112,4,128]{3,1,2,0:T(8,128)(2,1)S(1)}, u32[]{:S(2)}, u32[]{:S(2)}) collective-permute-start(bf16[2,112,4,128]{3,1,2,0:T(8,128)(2,1)S(1)} %get-tuple-element.416), channel_id=1, source_target_pairs={{0,2},{2,4},{4,6},{6,8},{8,10},{10,12},{12,14},{14,16},{16,18},{18... | collective-permute-start | bytes 688136 | tf_op jit(solution)/shard_map/while/body/eval_jaxpr/ppermute | solution.py:15
  132.8 8.1 %collective-permute-start.1 = (bf16[2,112,4,128]{3,1,2,0:T(8,128)(2,1)S(1)}, bf16[2,112,4,128]{3,1,2,0:T(8,128)(2,1)S(1)}, u32[]{:S(2)}, u32[]{:S(2)}) collective-permute-start(bf16[2,112,4,128]{3,1,2,0:T(8,128)(2,1)S(1)} %collective-permute-done), channel_id=1, source_target_pairs={{0,2},{2,4},{4,6},{6,8},{8,10},{10,12},{12,14},{14,16},{16,18},{18... | collective-permute-start | bytes 688136 | tf_op jit(solution)/shard_map/while/body/eval_jaxpr/ppermute | solution.py:15
  141.0 8.1 %collective-permute-start = (bf16[2,112,4,128]{3,1,2,0:T(8,128)(2,1)S(1)}, bf16[2,112,4,128]{3,1,2,0:T(8,128)(2,1)S(1)}, u32[]{:S(2)}, u32[]{:S(2)}) collective-permute-start(bf16[2,112,4,128]{3,1,2,0:T(8,128)(2,1)S(1)} %get-tuple-element.416), channel_id=1, source_target_pairs={{0,2},{2,4},{4,6},{6,8},{8,10},{10,12},{12,14},{14,16},{16,18},{18... | collective-permute-start | bytes 688136 | tf_op jit(solution)/shard_map/while/body/eval_jaxpr/ppermute | solution.py:15
  157.9 8.1 %collective-permute-start.1 = (bf16[2,112,4,128]{3,1,2,0:T(8,128)(2,1)S(1)}, bf16[2,112,4,128]{3,1,2,0:T(8,128)(2,1)S(1)}, u32[]{:S(2)}, u32[]{:S(2)}) collective-permute-start(bf16[2,112,4,128]{3,1,2,0:T(8,128)(2,1)S(1)} %collective-permute-done), channel_id=1, source_target_pairs={{0,2},{2,4},{4,6},{6,8},{8,10},{10,12},{12,14},{14,16},{16,18},{18... | collective-permute-start | bytes 688136 | tf_op jit(solution)/shard_map/while/body/eval_jaxpr/ppermute | solution.py:15
  166.0 8.1 %collective-permute-start = (bf16[2,112,4,128]{3,1,2,0:T(8,128)(2,1)S(1)}, bf16[2,112,4,128]{3,1,2,0:T(8,128)(2,1)S(1)}, u32[]{:S(2)}, u32[]{:S(2)}) collective-permute-start(bf16[2,112,4,128]{3,1,2,0:T(8,128)(2,1)S(1)} %get-tuple-element.416), channel_id=1, source_target_pairs={{0,2},{2,4},{4,6},{6,8},{8,10},{10,12},{12,14},{14,16},{16,18},{18... | collective-permute-start | bytes 688136 | tf_op jit(solution)/shard_map/while/body/eval_jaxpr/ppermute | solution.py:15
  182.9 8.1 %collective-permute-start.1 = (bf16[2,112,4,128]{3,1,2,0:T(8,128)(2,1)S(1)}, bf16[2,112,4,128]{3,1,2,0:T(8,128)(2,1)S(1)}, u32[]{:S(2)}, u32[]{:S(2)}) collective-permute-start(bf16[2,112,4,128]{3,1,2,0:T(8,128)(2,1)S(1)} %collective-permute-done), channel_id=1, source_target_pairs={{0,2},{2,4},{4,6},{6,8},{8,10},{10,12},{12,14},{14,16},{16,18},{18... | collective-permute-start | bytes 688136 | tf_op jit(solution)/shard_map/while/body/eval_jaxpr/ppermute | solution.py:15
  191.1 8.1 %collective-permute-start = (bf16[2,112,4,128]{3,1,2,0:T(8,128)(2,1)S(1)}, bf16[2,112,4,128]{3,1,2,0:T(8,128)(2,1)S(1)}, u32[]{:S(2)}, u32[]{:S(2)}) collective-permute-start(bf16[2,112,4,128]{3,1,2,0:T(8,128)(2,1)S(1)} %get-tuple-element.416), channel_id=1, source_target_pairs={{0,2},{2,4},{4,6},{6,8},{8,10},{10,12},{12,14},{14,16},{16,18},{18... | collective-permute-start | bytes 688136 | tf_op jit(solution)/shard_map/while/body/eval_jaxpr/ppermute | solution.py:15
  208.0 8.1 %collective-permute-start.1 = (bf16[2,112,4,128]{3,1,2,0:T(8,128)(2,1)S(1)}, bf16[2,112,4,128]{3,1,2,0:T(8,128)(2,1)S(1)}, u32[]{:S(2)}, u32[]{:S(2)}) collective-permute-start(bf16[2,112,4,128]{3,1,2,0:T(8,128)(2,1)S(1)} %collective-permute-done), channel_id=1, source_target_pairs={{0,2},{2,4},{4,6},{6,8},{8,10},{10,12},{12,14},{14,16},{16,18},{18... | collective-permute-start | bytes 688136 | tf_op jit(solution)/shard_map/while/body/eval_jaxpr/ppermute | solution.py:15
where the time goes:
time: 261 us
  matrix products  101 us (39%)
  waiting for transfers between devices  78.8 us (30%)
  other arithmetic  42.1 us (16%)
  blocking collectives  19.7 us (8%)
  local copies, waits for them, and re-layouts  17.9 us (7%)
    ppermute x16, waiting for transfers between devices, passed_along(): return lax.ppermute(value, axis, pairs)  78.8 us
    dot_general x16, matrix products, block_partial(): jnp.einsum('gjqk,kgd->qgjd', weights.astype(jnp.bfloat16), value_block, p...  78.5 us
    dot_general x16, matrix products, block_partial(): jnp.einsum('qgjd,kgd->gjqk', query_block, key_block, preferred_element_ty...  22.5 us
    reduce_sum x1, other arithmetic, merge_parts(): numer = jnp.sum(factors[..., None] * parts.astype(jnp.float32), axis=0)  20 us
    all_to_all x1, blocking collectives, per_device(): lax.all_to_all(merged, 'head', split_axis=0, concat_axis=1, tiled=True)  19.7 us
    reduce_sum x8, other arithmetic, block_partial(): totals = jnp.sum(weights, axis=-1)  18.7 us
    broadcast_in_dim x1, local copies, waits for them, and re-layouts, per_device(): jnp.zeros((cycle_size, row_count, kv_local, group, HEAD_DIM), jnp.bfloat16)  10.2 us
  transfers between devices with their start and end apart: 16, of which 16 were waited for; matrix products, arithmetic and copies ran while one was open for 20% of the time, Pallas kernels for 0%

commit v1 on v0

v1 whole, which is shorter than its diff:
```python
import functools
import math

import jax
import jax.numpy as jnp
from jax import lax
from jax.experimental import pallas as pl
from jax.experimental.pallas import tpu as pltpu
from jax.sharding import PartitionSpec as P

HEAD_DIM = 128
NEG_FLOOR = -1e30
MESH = pl.DeviceIdType.MESH
STACK = 4


def attend_kernel(
    n_ctx, n_head, q_ref, k_ref, v_ref, qpos_ref, kpos_ref, out_ref,
    kv, bias, obuf, own_sem, send_sem, recv_sem, osend_sem, orecv_sem, olocal_sem,
):
    rows = q_ref.shape[0]
    kv_local = k_ref.shape[1] // HEAD_DIM
    group = q_ref.shape[1] // HEAD_DIM // kv_local
    subs = group // STACK
    width = STACK * HEAD_DIM
    part = rows // n_head
    chips = n_ctx // 2
    deep = chips // 2
    n_keys = n_ctx * rows

    ctx = lax.axis_index("ctx")
    head = lax.axis_index("head")
    core = lax.rem(ctx, 2)
    chip = ctx // 2
    chip_z, chip_y = chip // 2, lax.rem(chip, 2)
    place = chip_z * (1 - chip_y) + (chips - 1 - chip_z) * chip_y

    def ctx_of(spot, which):
        spot = lax.rem(spot + 2 * chips, chips)
        far = spot // deep
        z = spot * (1 - far) + (chips - 1 - spot) * far
        return (2 * z + far) * 2 + which

    right, left, partner = ctx_of(place + 1, core), ctx_of(place - 1, core), ctx_of(place, 1 - core)

    def own_copies(g):
        cols = pl.ds(g * HEAD_DIM, HEAD_DIM)
        return (
            pltpu.make_async_copy(k_ref.at[:, cols], kv.at[g, ctx, 0], own_sem.at[g, 0]),
            pltpu.make_async_copy(v_ref.at[:, cols], kv.at[g, ctx, 1], own_sem.at[g, 1]),
        )

    for g in range(kv_local):
        for copy in own_copies(g):
            copy.start()

    barrier = pltpu.get_barrier_semaphore()
    for peer in (right, left, partner):
        pl.semaphore_signal(barrier, inc=1, device_id={"ctx": peer}, device_id_type=MESH)
    for hop in range(1, n_head):
        pl.semaphore_signal(
            barrier, inc=1, device_id={"head": lax.rem(head + hop, n_head)}, device_id_type=MESH
        )
    pl.semaphore_wait(barrier, 3 + n_head - 1)

    def ship(g, block, way, number, peer):
        return pltpu.make_async_remote_copy(
            src_ref=kv.at[g, block],
            dst_ref=kv.at[g, block],
            send_sem=send_sem.at[g, way, number],
            recv_sem=recv_sem.at[g, block],
            device_id={"ctx": peer},
            device_id_type=MESH,
        )

    def first_step(g):
        for copy in own_copies(g):
            copy.wait()
        ship(g, ctx, 0, 0, right).start()
        ship(g, ctx, 1, 0, left).start()
        ship(g, ctx, 2, 0, partner).start()

    def right_last(g):
        return deep - lax.rem(g, 2)

    def left_last(g):
        return chips - 1 - right_last(g)

    def later_step(g, step):
        @pl.when(step <= right_last(g))
        def _():
            block = ctx_of(place - step, core)
            ship(g, block, 0, step, right).wait_recv()

            @pl.when(step < right_last(g))
            def _():
                ship(g, block, 0, step, right).start()

            ship(g, block, 2, step, partner).start()

        @pl.when(step <= left_last(g))
        def _():
            block = ctx_of(place + step, core)
            ship(g, block, 1, step, left).wait_recv()

            @pl.when(step < left_last(g))
            def _():
                ship(g, block, 1, step, left).start()

            ship(g, block, 2, chips - step, partner).start()

    def partner_wait(g):
        def one(spot, carry):
            ship(g, ctx_of(spot, 1 - core), 2, 0, partner).wait_recv()
            return carry

        lax.fori_loop(0, chips, one, 0)

    for g in range(kv_local):
        first_step(g)

    bias[...] = jnp.where(kpos_ref[...] <= qpos_ref[...], 0.0, NEG_FLOOR)

    def initial(step, carry):
        later_step(0, step)
        return carry

    lax.fori_loop(1, deep + 1, initial, 0)
    partner_wait(0)

    ring_per_sub = -(-deep // subs)
    factor = HEAD_DIM ** (-0.5) * math.log2(math.e)
    ones = jnp.ones((n_keys, HEAD_DIM), jnp.bfloat16)

    def out_copy(index, peer_head):
        mine = pl.ds(pl.multiple_of((head * kv_local * subs + index) * width, width), width)
        return pltpu.make_async_remote_copy(
            src_ref=obuf.at[peer_head, index],
            dst_ref=out_ref.at[:, mine],
            send_sem=osend_sem.at[peer_head, index],
            recv_sem=orecv_sem.at[head, index],
            device_id={"head": peer_head},
            device_id_type=MESH,
        )

    def in_copy(index, from_head):
        theirs = pl.ds(pl.multiple_of((from_head * kv_local * subs + index) * width, width), width)
        return pltpu.make_async_remote_copy(
            src_ref=obuf.at[head, index],
            dst_ref=out_ref.at[:, theirs],
            send_sem=osend_sem.at[from_head, index],
            recv_sem=orecv_sem.at[from_head, index],
            device_id={"head": from_head},
            device_id_type=MESH,
        )

    def local_copy(index):
        mine = pl.ds(pl.multiple_of((head * kv_local * subs + index) * width, width), width)
        return pltpu.make_async_copy(
            obuf.at[head, index], out_ref.at[:, mine], olocal_sem.at[index]
        )

    def sub_step(index, carry):
        g, sub = index // subs, lax.rem(index, subs)

        @pl.when(g + 1 < kv_local)
        def _():
            for extra in range(ring_per_sub):
                step = sub * ring_per_sub + extra + 1

                @pl.when(step <= deep)
                def _():
                    later_step(g + 1, step)

        @pl.when(jnp.logical_and(g > 0, sub == 0))
        def _():
            partner_wait(g)

        keys = kv[g, :, 0].reshape(n_keys, HEAD_DIM)
        vals = jnp.concatenate([kv[g, :, 1].reshape(n_keys, HEAD_DIM), ones], axis=1)
        start = index * width
        queries = jnp.concatenate(
            [
                q_ref[:, pl.ds(pl.multiple_of(start + j * HEAD_DIM, HEAD_DIM), HEAD_DIM)]
                for j in range(STACK)
            ],
            axis=0,
        )
        scores = lax.dot_general(
            queries, keys, (((1,), (1,)), ((), ())), preferred_element_type=jnp.float32
        )
        scores = (scores.reshape(STACK, rows, n_keys) + bias[...][None]).reshape(STACK * rows, n_keys)
        row_max = jnp.max(scores, axis=1, keepdims=True)
        weights = jnp.exp2((scores - row_max) * factor).astype(jnp.bfloat16)
        both = jnp.dot(weights, vals, preferred_element_type=jnp.float32)
        result = both[:, :HEAD_DIM] / both[:, HEAD_DIM:]
        for j in range(STACK):
            for d in range(n_head):
                piece = result[j * rows + d * part : j * rows + (d + 1) * part]
                obuf[d, index, :, j * HEAD_DIM : (j + 1) * HEAD_DIM] = piece.astype(jnp.bfloat16)
        for hop in range(1, n_head):
            out_copy(index, lax.rem(head + hop, n_head)).start()
        local_copy(index).start()
        return carry

    lax.fori_loop(0, kv_local * subs, sub_step, 0)

    def finish(index, carry):
        for hop in range(1, n_head):
            peer = lax.rem(head + hop, n_head)
            out_copy(index, peer).wait_send()
            in_copy(index, peer).wait_recv()
        local_copy(index).wait()
        return carry

    lax.fori_loop(0, kv_local * subs, finish, 0)

    def drain(g, carry):
        def right_one(step, inner):
            ship(g, ctx, 0, step, right).wait_send()
            return inner

        def left_one(step, inner):
            ship(g, ctx, 1, step, left).wait_send()
            return inner

        def partner_one(step, inner):
            ship(g, ctx, 2, step, partner).wait_send()
            return inner

        lax.fori_loop(0, right_last(g), right_one, 0)
        lax.fori_loop(0, left_last(g), left_one, 0)
        lax.fori_loop(0, chips, partner_one, 0)
        return carry

    lax.fori_loop(0, kv_local, drain, 0)


def per_device(n_ctx, n_head, queries, keys, values, span_pos):
    rows = queries.shape[0]
    span_len = rows // 2
    kv_local = keys.shape[1] // HEAD_DIM
    subs = queries.shape[1] // HEAD_DIM // kv_local // STACK
    chips = n_ctx // 2
    positions = (
        span_pos[:, None] * span_len + jnp.arange(span_len, dtype=jnp.int32)[None, :]
    ).reshape(-1)
    mine = lax.dynamic_slice_in_dim(positions, lax.axis_index("ctx") * rows, rows)
    vmem = pl.BlockSpec(memory_space=pltpu.VMEM)
    n_sub = kv_local * subs
    return pl.pallas_call(
        functools.partial(attend_kernel, n_ctx, n_head),
        out_shape=jax.ShapeDtypeStruct((rows // n_head, queries.shape[1] * n_head), jnp.bfloat16),
        in_specs=[vmem] * 5,
        out_specs=pl.BlockSpec(memory_space=pl.ANY),
        scratch_shapes=[
            pltpu.VMEM((kv_local, n_ctx, 2, rows, HEAD_DIM), jnp.bfloat16),
            pltpu.VMEM((rows, n_ctx * rows), jnp.float32),
            pltpu.VMEM((n_head, n_sub, rows // n_head, STACK * HEAD_DIM), jnp.bfloat16),
            pltpu.SemaphoreType.DMA((kv_local, 2)),
            pltpu.SemaphoreType.DMA((kv_local, 3, chips)),
            pltpu.SemaphoreType.DMA((kv_local, n_ctx)),
            pltpu.SemaphoreType.DMA((n_head, n_sub)),
            pltpu.SemaphoreType.DMA((n_head, n_sub)),
            pltpu.SemaphoreType.DMA((n_sub,)),
        ],
        compiler_params=pltpu.CompilerParams(
            collective_id=0, has_side_effects=True, vmem_limit_bytes=60 * 1024 * 1024
        ),
    )(queries, keys, values, mine[:, None], positions[None, :])


def solution(mesh):
    in_specs = (P("ctx", "head"), P("ctx", "head"), P("ctx", "head"), P())
    out_specs = P(("ctx", "head"), None)
    return jax.shard_map(
        functools.partial(per_device, mesh.shape["ctx"], mesh.shape["head"]),
        mesh=mesh, in_specs=in_specs, out_specs=out_specs, check_vma=False,
    )
```

time: 261 us -> 76.9 us (0.29)
  matrix products: 101 us -> 0 us
  waiting for transfers between devices: 78.8 us -> 0 us
  Pallas kernels: 0 us -> 71.6 us
  other arithmetic: 42.1 us -> 0.73 us
  blocking collectives: 19.7 us -> 0 us
  local copies, waits for them, and re-layouts: 17.9 us -> 4.43 us
    dot_general x32 -> x0, matrix products: 101 us -> none  [the longest x16 78.5 us: block_partial(): jnp.einsum('gjqk,kgd->qgjd', weights.astype(jnp.bfloat16), value_block, p...]
    ppermute x16 -> x0, waiting for transfers between devices: 78.8 us -> none  [passed_along(): return lax.ppermute(value, axis, pairs)]
    pallas_call x0 -> x1, Pallas kernels: none -> 71.6 us  [per_device(): pl.pallas_call(functools.partial(attend_kernel, n_ctx, n_head), out_shape...]
    reduce_sum x10 -> x0, other arithmetic: 38.8 us -> none  [the longest x1 20 us: merge_parts(): numer = jnp.sum(factors[..., None] * parts.astype(jnp.float32), axis=0)]
    all_to_all x1 -> x0, blocking collectives: 19.7 us -> none  [per_device(): lax.all_to_all(merged, 'head', split_axis=0, concat_axis=1, tiled=True)]
    broadcast_in_dim x2, local copies, waits for them, and re-layouts: 10.2 us -> 0.81 us  [per_device(): mine[:, None]]
  transfers between devices with their start and end apart: 16 -> 0, of which waited for: 16 -> 0; matrix products, arithmetic and copies ran while one was open for 20% -> 0% of each run, Pallas kernels for 0% -> 0%
where the time goes in v1:
time: 76.9 us; the launch traced here: 76.7 us
  Pallas kernels  71.6 us (93%)
  local copies, waits for them, and re-layouts  4.43 us (6%)
    pallas_call x1, Pallas kernels, per_device(): pl.pallas_call(functools.partial(attend_kernel, n_ctx, n_head), out_shape...  71.6 us
    unnamed x1, local copies, waits for them, and re-layouts  2.85 us

profile of v1, /device:TPU:0, one launch (start us, length us, event | category | flops | bytes accessed | tf_op | source)
XLA Modules:
  0.0 76.7 jit_solution(2813864040628147687)
XLA Ops:
  0.0 0.7 broadcast_multiply_fusion
  0.7 0.1 iota_add_fusion
  0.7 0.7 add.35.kpos_ref
  1.4 0.1 add.33
  1.5 0.1 dynamic-slice_bitcast_fusion
  1.6 0.7 copy.5.qpos_ref
  2.3 71.6 %shard_map.46 = bf16[56,16384]{1,0:T(8,128)(2,1)} custom-call(bf16[112,8192]{1,0:T(8,128)(2,1)} %q_ref.1, bf16[112,512]{1,0:T(8,128)(2,1)} %k_ref.1, bf16[112,512]{1,0:T(8,128)(2,1)} %v_ref.1, s32[112,1]{1,0:T(8,128)} %copy.5.qpos_ref, s32[1,1792]{1,0:T(1,128)} %add.35.kpos_ref), custom_call_target="tpu_custom_call" | custom-call | tf_op jit(solution)/shard_map/pallas_call | solution.py:251
  73.9 2.8 %copy.7 = bf16[56,16384]{1,0:T(8,128)(2,1)} copy(bf16[56,16384]{1,0:T(8,128)(2,1)} %shard_map.46) | data formatting | bytes 3670016

commit v2 on v1

--- a/solution.py
+++ b/solution.py
@@ -11,11 +11,12 @@
 HEAD_DIM = 128
 NEG_FLOOR = -1e30
 MESH = pl.DeviceIdType.MESH
-STACK = 4
+STACK = 8
+UNIT = 2
 
 
 def attend_kernel(
-    n_ctx, n_head, q_ref, k_ref, v_ref, qpos_ref, kpos_ref, out_ref,
+    n_ctx, n_head, q_ref, k_ref, v_ref, span_ref, out_ref,
     kv, bias, obuf, own_sem, send_sem, recv_sem, osend_sem, orecv_sem, olocal_sem,
 ):
     rows = q_ref.shape[0]
@@ -81,7 +82,7 @@
         ship(g, ctx, 2, 0, partner).start()
 
     def right_last(g):
-        return deep - lax.rem(g, 2)
+        return deep - g % 2
 
     def left_last(g):
         return chips - 1 - right_last(g)
@@ -119,16 +120,31 @@
     for g in range(kv_local):
         first_step(g)
 
-    bias[...] = jnp.where(kpos_ref[...] <= qpos_ref[...], 0.0, NEG_FLOOR)
-
-    def initial(step, carry):
-        later_step(0, step)
+    span_len = rows // 2
+    row = lax.broadcasted_iota(jnp.int32, (rows, 1), 0)
+    q_pos = row + jnp.where(
+        row < span_len,
+        span_ref[2 * ctx] * span_len,
+        (span_ref[2 * ctx + 1] - 1) * span_len,
+    )
+    col = lax.broadcasted_iota(jnp.int32, (1, n_keys), 1)
+    k_pos = col
+    for span in range(2 * n_ctx):
+        k_pos = jnp.where(col >= span * span_len, col + (span_ref[span] - span) * span_len, k_pos)
+    bias[...] = jnp.where(k_pos <= q_pos, 0.0, NEG_FLOOR)
+
+    def tick(turn):
+        for g in range(kv_local):
+            @pl.when(jnp.logical_and(turn - g >= 1, turn - g <= deep))
+            def _():
+                later_step(g, turn - g)
+
+    def initial(turn, carry):
+        tick(turn)
         return carry
 
     lax.fori_loop(1, deep + 1, initial, 0)
-    partner_wait(0)
-
-    ring_per_sub = -(-deep // subs)
+
     factor = HEAD_DIM ** (-0.5) * math.log2(math.e)
     ones = jnp.ones((n_keys, HEAD_DIM), jnp.bfloat16)
 
@@ -163,44 +179,52 @@
     def sub_step(index, carry):
         g, sub = index // subs, lax.rem(index, subs)
 
-        @pl.when(g + 1 < kv_local)
-        def _():
-            for extra in range(ring_per_sub):
-                step = sub * ring_per_sub + extra + 1
-
-                @pl.when(step <= deep)
-                def _():
-                    later_step(g + 1, step)
-
-        @pl.when(jnp.logical_and(g > 0, sub == 0))
+        @pl.when(sub == 0)
         def _():
             partner_wait(g)
 
         keys = kv[g, :, 0].reshape(n_keys, HEAD_DIM)
         vals = jnp.concatenate([kv[g, :, 1].reshape(n_keys, HEAD_DIM), ones], axis=1)
         start = index * width
-        queries = jnp.concatenate(
-            [
-                q_ref[:, pl.ds(pl.multiple_of(start + j * HEAD_DIM, HEAD_DIM), HEAD_DIM)]
-                for j in range(STACK)
-            ],
-            axis=0,
-        )
-        scores = lax.dot_general(
-            queries, keys, (((1,), (1,)), ((), ())), preferred_element_type=jnp.float32
-        )
-        scores = (scores.reshape(STACK, rows, n_keys) + bias[...][None]).reshape(STACK * rows, n_keys)
-        row_max = jnp.max(scores, axis=1, keepdims=True)
-        weights = jnp.exp2((scores - row_max) * factor).astype(jnp.bfloat16)
-        both = jnp.dot(weights, vals, preferred_element_type=jnp.float32)
-        result = both[:, :HEAD_DIM] / both[:, HEAD_DIM:]
-        for j in range(STACK):
-            for d in range(n_head):
-                piece = result[j * rows + d * part : j * rows + (d + 1) * part]
-                obuf[d, index, :, j * HEAD_DIM : (j + 1) * HEAD_DIM] = piece.astype(jnp.bfloat16)
+        groups = STACK // UNIT
+
+        def make_scores(u):
+            queries = jnp.concatenate(
+                [
+                    q_ref[:, pl.ds(pl.multiple_of(start + (u * UNIT + j) * HEAD_DIM, HEAD_DIM), HEAD_DIM)]
+                    for j in range(UNIT)
+                ],
+                axis=0,
+            )
+            scores = lax.dot_general(
+                queries, keys, (((1,), (1,)), ((), ())), preferred_element_type=jnp.float32
+            )
+            return (scores.reshape(UNIT, rows, n_keys) + bias[...][None]).reshape(UNIT * rows, n_keys)
+
+        def finish_unit(u, weights):
+            both = jnp.dot(weights, vals, preferred_element_type=jnp.float32)
+            result = both[:, :HEAD_DIM] / both[:, HEAD_DIM:]
+            for j in range(UNIT):
+                for d in range(n_head):
+                    piece = result[j * rows + d * part : j * rows + (d + 1) * part]
+                    at = (u * UNIT + j) * HEAD_DIM
+                    obuf[d, index, :, at : at + HEAD_DIM] = piece.astype(jnp.bfloat16)
+
+        scores = make_scores(0)
+        for u in range(groups):
+            following = make_scores(u + 1) if u + 1 < groups else None
+            row_max = jnp.max(scores, axis=1, keepdims=True)
+            weights = jnp.exp2((scores - row_max) * factor).astype(jnp.bfloat16)
+            finish_unit(u, weights)
+            scores = following
         for hop in range(1, n_head):
             out_copy(index, lax.rem(head + hop, n_head)).start()
         local_copy(index).start()
+
+        @pl.when(index + 1 < kv_local)
+        def _():
+            tick(deep + 1 + index)
+
         return carry
 
     lax.fori_loop(0, kv_local * subs, sub_step, 0)
@@ -238,20 +262,15 @@
 
 def per_device(n_ctx, n_head, queries, keys, values, span_pos):
     rows = queries.shape[0]
-    span_len = rows // 2
     kv_local = keys.shape[1] // HEAD_DIM
     subs = queries.shape[1] // HEAD_DIM // kv_local // STACK
     chips = n_ctx // 2
-    positions = (
-        span_pos[:, None] * span_len + jnp.arange(span_len, dtype=jnp.int32)[None, :]
-    ).reshape(-1)
-    mine = lax.dynamic_slice_in_dim(positions, lax.axis_index("ctx") * rows, rows)
     vmem = pl.BlockSpec(memory_space=pltpu.VMEM)
     n_sub = kv_local * subs
     return pl.pallas_call(
         functools.partial(attend_kernel, n_ctx, n_head),
         out_shape=jax.ShapeDtypeStruct((rows // n_head, queries.shape[1] * n_head), jnp.bfloat16),
-        in_specs=[vmem] * 5,
+        in_specs=[vmem] * 3 + [pl.BlockSpec(memory_space=pltpu.SMEM)],
         out_specs=pl.BlockSpec(memory_space=pl.ANY),
         scratch_shapes=[
             pltpu.VMEM((kv_local, n_ctx, 2, rows, HEAD_DIM), jnp.bfloat16),
@@ -267,7 +286,7 @@
         compiler_params=pltpu.CompilerParams(
             collective_id=0, has_side_effects=True, vmem_limit_bytes=60 * 1024 * 1024
         ),
-    )(queries, keys, values, mine[:, None], positions[None, :])
+    )(queries, keys, values, span_pos)
 
 
 def solution(mesh):

time: 76.9 us -> 56 us (0.73)
  Pallas kernels: 71.6 us -> 52.9 us
  local copies, waits for them, and re-layouts: 4.43 us -> 2.85 us
    pallas_call x1, Pallas kernels: 71.6 us -> 52.9 us  [per_device(): pl.pallas_call(functools.partial(attend_kernel, n_ctx, n_head), out_shape...]
    broadcast_in_dim x2 -> x0, local copies, waits for them, and re-layouts: 0.81 us -> none  [per_device(): mine[:, None]]
    add x2 -> x0, local copies, waits for them, and re-layouts: 0.77 us -> none  [per_device(): span_pos[:, None] * span_len]
where the time goes in v2:
time: 56 us; the launch traced here: 55.8 us
  Pallas kernels  52.9 us (94%)
  local copies, waits for them, and re-layouts  2.85 us (5%)
    pallas_call x1, Pallas kernels, per_device(): pl.pallas_call(functools.partial(attend_kernel, n_ctx, n_head), out_shape...  52.9 us
    unnamed x1, local copies, waits for them, and re-layouts  2.85 us

profile of v2, /device:TPU:0, one launch (start us, length us, event | category | flops | bytes accessed | tf_op | source)
XLA Modules:
  0.0 55.8 jit_solution(18282504751006105858)
XLA Ops:
  0.0 52.9 %shard_map.46 = bf16[56,16384]{1,0:T(8,128)(2,1)} custom-call(bf16[112,8192]{1,0:T(8,128)(2,1)} %q_ref.1, bf16[112,512]{1,0:T(8,128)(2,1)} %k_ref.1, bf16[112,512]{1,0:T(8,128)(2,1)} %v_ref.1, s32[32]{0:T(128)} %span_ref.1), custom_call_target="tpu_custom_call" | custom-call | tf_op jit(solution)/shard_map/pallas_call | solution.py:270
  53.0 2.8 %copy.6 = bf16[56,16384]{1,0:T(8,128)(2,1)} copy(bf16[56,16384]{1,0:T(8,128)(2,1)} %shard_map.46) | data formatting | bytes 3670016

commit v3 on v2

--- a/solution.py
+++ b/solution.py
@@ -11,7 +11,7 @@
 HEAD_DIM = 128
 NEG_FLOOR = -1e30
 MESH = pl.DeviceIdType.MESH
-STACK = 8
+STACK = 16
 UNIT = 2
 
 

time: 56 us -> 55.2 us (0.986)
  Pallas kernels: 52.9 us -> 52.2 us
    pallas_call x1, Pallas kernels: 52.9 us -> 52.2 us  [per_device(): pl.pallas_call(functools.partial(attend_kernel, n_ctx, n_head), out_shape...]
where the time goes in v3:
time: 55.2 us; the launch traced here: 55 us
  Pallas kernels  52.2 us (95%)
  local copies, waits for them, and re-layouts  2.85 us (5%)
    pallas_call x1, Pallas kernels, per_device(): pl.pallas_call(functools.partial(attend_kernel, n_ctx, n_head), out_shape...  52.2 us
    unnamed x1, local copies, waits for them, and re-layouts  2.85 us

profile of v3, /device:TPU:0, one launch (start us, length us, event | category | flops | bytes accessed | tf_op | source)
XLA Modules:
  0.0 55.0 jit_solution(17405767586059585145)
XLA Ops:
  0.0 52.2 %shard_map.46 = bf16[56,16384]{1,0:T(8,128)(2,1)} custom-call(bf16[112,8192]{1,0:T(8,128)(2,1)} %q_ref.1, bf16[112,512]{1,0:T(8,128)(2,1)} %k_ref.1, bf16[112,512]{1,0:T(8,128)(2,1)} %v_ref.1, s32[32]{0:T(128)} %span_ref.1), custom_call_target="tpu_custom_call" | custom-call | tf_op jit(solution)/shard_map/pallas_call | solution.py:270
  52.2 2.8 %copy.6 = bf16[56,16384]{1,0:T(8,128)(2,1)} copy(bf16[56,16384]{1,0:T(8,128)(2,1)} %shard_map.46) | data formatting | bytes 3670016
